TPU v7x, 32 devices: a whole 2x2x4 slice. The times are simulated.
32 devices in a mesh: dp: 16 (over z, y, core), tensor: 2 (over x).
Axes of the slice: x: 2, y: 2, z: 4, core: 2. Of those that a mesh axis runs over, the one named last changes fastest.
Arguments:
- noisy_sample: float32 [2048, 28], P('dp'), may hold values from -5 to 5
- timestep: int32 [2048], P('dp'), may hold values from 0 to 99
- noise: float32 [2048, 28], P('dp'), may hold values from -5 to 5
- obs_feat: bfloat16 [2048, 1024], P('dp'), may hold values from -6 to 6
- step_w1: bfloat16 [256, 1024], replicated, may hold values from -0.75 to 0.75
- step_w2: bfloat16 [1024, 256], replicated, may hold values from -0.25 to 0.25
- film_weight: bfloat16 [1280, 2, 4096], P('dp', None, 'tensor'), may hold values from -0.25 to 0.25
- conv_in_w: bfloat16 [5, 7, 4096], P(None, None, 'tensor'), may hold values from -1 to 1
- residual_w: bfloat16 [7, 4096], P(None, 'tensor'), may hold values from -2 to 2
- conv_mid_w: bfloat16 [5, 4096, 4096], P(None, 'dp', 'tensor'), may hold values from -0.0390625 to 0.0390625
- out_w: bfloat16 [4096, 7], P('tensor'), may hold values from -0.1875 to 0.1875
- gain_one: float32 [4096], P('tensor'), may hold values from 0.4 to 1.6
- gain_two: float32 [4096], P('tensor'), may hold values from 0.4 to 1.6
Outputs:
- predicted_noise: float32 [2048, 28], P('dp')
- denoised: float32 [2048, 28], P('dp')
All inputs are finite; a program needn't handle non-finite values.
Results may differ from a plain program's by a relative error of at most 0.0046.
Values may be sent and summed in bfloat16 or wider, within the bound.
A program may use at most 192 MiB of HBM per device.

v0:
```python
import math

import jax
import jax.numpy as jnp
from jax import lax
from jax.sharding import PartitionSpec as P

C = 4096
ACT = 7
HORIZON = 4
TAPS = 5
GROUPS = 8
STEP = 256
TRAIN_STEPS = 100


def plan():
    pos = jnp.arange(TRAIN_STEPS + 1, dtype=jnp.float32) / TRAIN_STEPS
    curve = jnp.cos((pos + 0.008) / 1.008 * (math.pi / 2)) ** 2
    betas = jnp.minimum(1.0 - curve[1:] / curve[:-1], 0.999)
    return jnp.cumprod(1.0 - betas)


def lookup(table, steps):
    onehot = (steps[:, None] == jnp.arange(table.shape[0], dtype=jnp.int32)[None, :]).astype(
        jnp.float32
    )
    return jnp.sum(onehot * table[None, :], axis=1)


def mish(value):
    return value * jnp.tanh(jax.nn.softplus(value))


def sinusoid(steps):
    half = STEP // 2
    freqs = jnp.exp(jnp.arange(half, dtype=jnp.float32) * (-math.log(10000.0) / (half - 1)))
    angles = steps.astype(jnp.float32)[:, None] * freqs[None, :]
    return jnp.concatenate([jnp.sin(angles), jnp.cos(angles)], axis=1)


def convolve(acts, weight):
    count, length, inner = acts.shape
    padded = jnp.pad(acts, ((0, 0), (2, 2), (0, 0)))
    total = jnp.zeros((count * length, weight.shape[2]), jnp.float32)
    for shift in range(TAPS):
        window = padded[:, shift : shift + length, :].reshape(count * length, inner)
        total = total + jnp.dot(window, weight[shift], preferred_element_type=jnp.float32)
    return total.reshape(count, length, weight.shape[2])


def group_norm(hidden, gain):
    count, length, width = hidden.shape
    groups = GROUPS * width // C
    split = hidden.reshape(count, length, groups, width // groups)
    mean = jnp.mean(split, axis=(1, 3), keepdims=True)
    var = jnp.mean((split - mean) ** 2, axis=(1, 3), keepdims=True)
    normed = ((split - mean) / jnp.sqrt(var + 1e-05)).reshape(count, length, width)
    return normed * gain[None, None, :]


def denoise_step(sample, eps, noise, steps):
    alpha_bar = plan()
    now = lookup(alpha_bar, steps)[:, None]
    before = jnp.where(steps > 0, lookup(alpha_bar, jnp.maximum(steps - 1, 0)), 1.0)[:, None]
    beta_prod = 1.0 - now
    cur_alpha = now / before
    cur_beta = 1.0 - cur_alpha
    start = jnp.clip((sample - jnp.sqrt(beta_prod) * eps) / jnp.sqrt(now), -1.0, 1.0)
    mean = (
        jnp.sqrt(before) * cur_beta / beta_prod * start
        + jnp.sqrt(cur_alpha) * (1.0 - before) / beta_prod * sample
    )
    spread = jnp.sqrt((1.0 - before) / beta_prod * cur_beta)
    return mean + spread * noise


def channel_mix(acts, weight):
    rows = lax.all_gather(weight, "dp", axis=1, tiled=True)
    return convolve(lax.all_gather(acts, "tensor", axis=2, tiled=True), rows)


def body(
    noisy_sample,
    timestep,
    noise,
    obs_feat,
    step_w1,
    step_w2,
    film_weight,
    conv_in_w,
    residual_w,
    conv_mid_w,
    out_w,
    gain_one,
    gain_two,
):
    count = noisy_sample.shape[0]
    local_width = conv_in_w.shape[2]
    sample_b = noisy_sample.reshape(count, HORIZON, ACT).astype(jnp.bfloat16)
    sinus = sinusoid(timestep).astype(jnp.bfloat16)
    step_hidden = mish(jnp.dot(sinus, step_w1, preferred_element_type=jnp.float32)).astype(
        jnp.bfloat16
    )
    step_feat = jnp.dot(step_hidden, step_w2, preferred_element_type=jnp.float32)
    cond = mish(jnp.concatenate([step_feat, obs_feat.astype(jnp.float32)], axis=1)).astype(
        jnp.bfloat16
    )
    piece = lax.all_gather(film_weight, "dp", axis=0, tiled=True)
    flat = piece.reshape(piece.shape[0], 2 * local_width)
    film = jnp.dot(cond, flat, preferred_element_type=jnp.float32)
    scale = film[:, :local_width]
    shift = film[:, local_width:]
    first = mish(group_norm(convolve(sample_b, conv_in_w), gain_one))
    act_one = (scale[:, None, :] * first + shift[:, None, :]).astype(jnp.bfloat16)
    skip = jnp.dot(
        sample_b.reshape(count * HORIZON, ACT), residual_w, preferred_element_type=jnp.float32
    ).reshape(count, HORIZON, local_width)
    act_two = (mish(group_norm(channel_mix(act_one, conv_mid_w), gain_two)) + skip).astype(
        jnp.bfloat16
    )
    partial_eps = jnp.dot(
        act_two.reshape(count * HORIZON, local_width), out_w, preferred_element_type=jnp.float32
    )
    eps = lax.psum(partial_eps, "tensor").reshape(count, HORIZON * ACT)
    denoised = denoise_step(noisy_sample, eps, noise, timestep)
    return (eps, denoised)


def solution(mesh):
    return jax.shard_map(
        body,
        mesh=mesh,
        in_specs=(
            P("dp", None),
            P("dp"),
            P("dp", None),
            P("dp", None),
            P(),
            P(),
            P("dp", None, "tensor"),
            P(None, None, "tensor"),
            P(None, "tensor"),
            P(None, "dp", "tensor"),
            P("tensor", None),
            P("tensor"),
            P("tensor"),
        ),
        out_specs=(P("dp", None), P("dp", None)),
        check_vma=False,
    )
```

profile of v0, /device:TPU:0, one launch (start us, length us, event | category | flops | bytes accessed | tf_op | source)
XLA Modules:
  0.0 714.8 jit_solution(10781574356708142810)
XLA Ops:
  7.2 0.7 all-gather.4.cloned.1.call-update
  8.0 0.7 convert_element_type.41
  8.9 0.5 copy-done.12
  11.5 1.5 fusion.43
  13.0 0.8 fusion.47
  13.8 0.8 fusion.49
  14.5 0.7 fusion.45
  15.2 3.2 add_add_fusion.1
  18.4 6.2 reshape_reshape.11
  24.6 5.4 reshape_reshape.10
  30.0 2.8 reduce_sum.54
  32.9 3.5 multiply_reduce_fusion.1
  37.9 1.6 fusion.27
  39.6 61.0 %all-gather.4.cloned.1.call-done = bf16[1280,2,2048]{2,1,0:T(2,128)(2,1)} async-done(((bf16[80,2,2048]{2,1,0:T(2,128)(2,1)}), bf16[1280,2,2048]{2,1,0:T(2,128)(2,1)}) %all-gather.4.cloned.1.call-update) | async-done | bytes 10485776 | tf_op jit(solution)/shard_map/all_gather | solution.py:109
  100.6 14.6 %copy.95 = bf16[160,8,2,2048]{3,1,2,0:T(8,128)(2,1)} copy(bf16[160,8,2,2048]{3,2,1,0:T(2,128)(2,1)} %bitcast.74) | data formatting | bytes 20971520
  115.2 6.3 fusion.24
  121.7 1.9 copy-done.2
  123.7 5.3 fusion.9
  129.0 0.7 all-gather.8.cloned.1.call-update
  130.4 53.8 %all-gather.6.cloned.1.call-done = bf16[128,4,4096]{2,0,1:T(8,128)(2,1)} async-done(((bf16[128,4,2048]{2,0,1:T(8,128)(2,1)}), bf16[128,4,4096]{2,0,1:T(8,128)(2,1)}) %all-gather.6.cloned.1.call-update) | async-done | bytes 4194320 | tf_op jit(solution)/shard_map/all_gather | solution.py:80
  184.1 8.4 %pad_slice_fusion.3 = (bf16[128,4,4096]{2,0,1:T(8,128)(2,1)}, bf16[128,4,4096]{2,0,1:T(8,128)(2,1)}, bf16[128,4,4096]{2,0,1:T(8,128)(2,1)}, bf16[128,4,4096]{2,0,1:T(8,128)(2,1)S(1)}) fusion(bf16[128,4,4096]{2,0,1:T(8,128)(2,1)} %all-gather.6.cloned.1.call-done), kind=kLoop, calls=%fused_computation.15 | loop fusion | bytes 20971520 | tf_op jit(solution)/shard_map/slice | solution.py:47
  192.5 5.3 copy.88
  197.8 7.0 reshape.152
  204.8 7.5 %copy.87 = bf16[128,4,4096]{2,1,0:T(4,128)(2,1)} copy(bf16[128,4,4096]{2,0,1:T(8,128)(2,1)} %get-tuple-element.15) | data formatting | bytes 8388608 | tf_op jit(solution)/shard_map/slice | solution.py:47
  212.2 7.0 reshape.151
  219.2 7.5 %copy.85 = bf16[128,4,4096]{2,1,0:T(4,128)(2,1)} copy(bf16[128,4,4096]{2,0,1:T(8,128)(2,1)} %get-tuple-element.14) | data formatting | bytes 8388608 | tf_op jit(solution)/shard_map/slice | solution.py:47
  226.7 7.1 reshape.149
  233.8 7.5 %copy.86 = bf16[128,4,4096]{2,1,0:T(4,128)(2,1)} copy(bf16[128,4,4096]{2,0,1:T(8,128)(2,1)} %all-gather.6.cloned.1.call-done) | data formatting | bytes 8388608 | tf_op jit(solution)/shard_map/all_gather | solution.py:80
  241.3 7.0 reshape.150
  248.3 7.5 %copy.84 = bf16[128,4,4096]{2,1,0:T(4,128)(2,1)} copy(bf16[128,4,4096]{2,0,1:T(8,128)(2,1)} %get-tuple-element.13) | data formatting | bytes 8388608 | tf_op jit(solution)/shard_map/slice | solution.py:47
  255.8 7.0 reshape.148
  262.7 328.1 %all-gather.8.cloned.1.call-done = bf16[5,4096,2048]{2,1,0:T(8,128)(2,1)} async-done(((bf16[5,256,2048]{2,1,0:T(8,128)(2,1)}), bf16[5,4096,2048]{2,1,0:T(8,128)(2,1)}) %all-gather.8.cloned.1.call-update) | async-done | bytes 83886096 | tf_op jit(solution)/shard_map/all_gather | solution.py:79
  590.8 15.2 %fusion = f32[512,2048]{1,0:T(8,128)} fusion(bf16[512,4096]{1,0:T(8,128)(2,1)} %reshape.152, bf16[5,4096,2048]{2,1,0:T(8,128)(2,1)} %all-gather.8.cloned.1.call-done), kind=kOutput, calls=%fused_computation.1 | convolution fusion | flops 8589934592 | bytes 25165824 | tf_op jit(solution)/shard_map/dot_general | solution.py:48
  606.0 14.4 %fusion.1 = f32[512,2048]{1,0:T(8,128)} fusion(bf16[512,4096]{1,0:T(8,128)(2,1)S(1)} %copy-done.3, bf16[5,4096,2048]{2,1,0:T(8,128)(2,1)} %all-gather.8.cloned.1.call-done), kind=kOutput, calls=%fused_computation.3 | convolution fusion | flops 8589934592 | bytes 25165824 | tf_op jit(solution)/shard_map/dot_general | solution.py:48
  620.4 14.1 %fusion.3 = f32[512,2048]{1,0:T(8,128)} fusion(bf16[512,4096]{1,0:T(8,128)(2,1)S(1)} %copy-done.5, bf16[5,4096,2048]{2,1,0:T(8,128)(2,1)} %all-gather.8.cloned.1.call-done), kind=kOutput, calls=%fused_computation.7 | convolution fusion | flops 8589934592 | bytes 25165824 | tf_op jit(solution)/shard_map/dot_general | solution.py:48
  634.5 14.1 %fusion.2 = f32[512,2048]{1,0:T(8,128)} fusion(bf16[512,4096]{1,0:T(8,128)(2,1)S(1)} %copy-done.6, bf16[5,4096,2048]{2,1,0:T(8,128)(2,1)} %all-gather.8.cloned.1.call-done), kind=kOutput, calls=%fused_computation.5 | convolution fusion | flops 8589934592 | bytes 25165824 | tf_op jit(solution)/shard_map/dot_general | solution.py:48
  648.6 20.0 %add_add_fusion = f32[512,2048]{1,0:T(8,128)} fusion(f32[512,2048]{1,0:T(8,128)} %fusion, f32[512,2048]{1,0:T(8,128)} %fusion.1, f32[512,2048]{1,0:T(8,128)} %fusion.2, f32[512,2048]{1,0:T(8,128)} %fusion.3, bf16[512,4096]{1,0:T(8,128)(2,1)S(1)} %copy-done.7, bf16[5,4096,2048]{2,1,0:T(8,128)(2,1)} %all-gather.8.cloned.1.call-done), kind=kOutput, calls=%fused_computation.32 | convolution fusion | flops 8594128896 | bytes 41943040 | tf_op jit(solution)/shard_map/dot_general | solution.py:48
  668.6 6.1 reshape_reshape.13
  674.6 5.2 reshape_reshape.12
  679.8 2.8 reduce_sum.56
  682.6 3.4 multiply_reduce_fusion
  687.2 1.0 copy-done.4
  688.3 4.6 fusion.13
  692.9 1.6 copy.90
  694.5 2.1 reshape.153
  696.6 2.3 fusion.63
  699.0 8.1 %psum.7 = f32[128,28]{0,1:T(8,128)S(1)} all-reduce(f32[128,28]{0,1:T(8,128)S(1)} %copy.92), channel_id=1, replica_groups=mesh['dp'=16,'tensor'=2] {'tensor'}, use_global_device_ids=true, to_apply=%region_4.5 | all-reduce | flops 3584 | bytes 28672 | tf_op jit(solution)/shard_map/psum | solution.py:125
  707.2 0.6 multiply_add_fusion
  (80 shorter events, 6.1 us)
Async XLA Ops:
  7.2 30.7 %copy-start = (bf16[1024,256]{1,0:T(8,128)(2,1)S(1)}, bf16[1024,256]{1,0:T(8,128)(2,1)}, u32[]{:S(2)}) copy-start(bf16[1024,256]{1,0:T(8,128)(2,1)} %param.18) | copy-start | bytes 1572868
  7.2 5.8 copy-start.9
  7.2 93.4 %all-gather.4.cloned.1.call-start = ((), (), s32[]{:S(2)}) async-start(), calls=%async_computation | async-start | bytes 11141120 | tf_op jit(solution)/shard_map/all_gather | solution.py:109
  7.9 176.2 %all-gather.6.cloned.1.call-start = ((), (), s32[]{:S(2)}) async-start(), calls=%async_computation.1 | async-start | bytes 6291456 | tf_op jit(solution)/shard_map/all_gather | solution.py:80
  8.7 0.6 copy-start.12
  36.3 1.2 copy-start.8
  36.3 1.2 copy-start.16
  115.2 6.5 copy-start.15
  121.5 2.2 copy-start.2
  129.0 461.8 %all-gather.8.cloned.1.call-start = ((), (), s32[]{:S(2)}) async-start(), calls=%async_computation.2 | async-start | bytes 89128960 | tf_op jit(solution)/shard_map/all_gather | solution.py:79
  590.8 15.2 %copy-start.3 = (bf16[512,4096]{1,0:T(8,128)(2,1)S(1)}, bf16[512,4096]{1,0:T(8,128)(2,1)}, u32[]{:S(2)}) copy-start(bf16[512,4096]{1,0:T(8,128)(2,1)} %reshape.151) | copy-start | bytes 12582916
  606.0 14.4 %copy-start.5 = (bf16[512,4096]{1,0:T(8,128)(2,1)S(1)}, bf16[512,4096]{1,0:T(8,128)(2,1)}, u32[]{:S(2)}) copy-start(bf16[512,4096]{1,0:T(8,128)(2,1)} %reshape.149) | copy-start | bytes 12582916
  620.4 14.1 %copy-start.6 = (bf16[512,4096]{1,0:T(8,128)(2,1)S(1)}, bf16[512,4096]{1,0:T(8,128)(2,1)}, u32[]{:S(2)}) copy-start(bf16[512,4096]{1,0:T(8,128)(2,1)} %reshape.150) | copy-start | bytes 12582916
  634.5 14.1 %copy-start.7 = (bf16[512,4096]{1,0:T(8,128)(2,1)S(1)}, bf16[512,4096]{1,0:T(8,128)(2,1)}, u32[]{:S(2)}) copy-start(bf16[512,4096]{1,0:T(8,128)(2,1)} %reshape.148) | copy-start | bytes 12582916
  686.1 2.2 copy-start.4
  686.1 2.2 copy-start.13
  686.1 2.2 copy-start.17
  686.1 2.2 copy-start.19
  692.8 3.8 copy-start.18
  692.8 15.0 %copy-start.1 = (bf16[1024,256]{1,0:T(8,128)(2,1)S(1)}, bf16[1024,256]{1,0:T(8,128)(2,1)}, u32[]{:S(2)}) copy-start(bf16[1024,256]{1,0:T(8,128)(2,1)} %param.18) | copy-start | bytes 1572868
  694.5 12.7 %copy-start.10 = (f32[128,28]{0,1:T(8,128)S(1)}, f32[128,28]{0,1:T(8,128)}, u32[]{:S(2)}) copy-start(f32[128,28]{0,1:T(8,128)} %param.13) | copy-start | bytes 43012
  694.5 12.7 %copy-start.14 = (f32[128,28]{0,1:T(8,128)S(1)}, f32[128,28]{0,1:T(8,128)}, u32[]{:S(2)}) copy-start(f32[128,28]{0,1:T(8,128)} %param.15) | copy-start | bytes 43012
  707.2 0.6 copy-start.11
Sparse Core Ops, SparseCore 0:
  10.3 90.2 all-gather.3
  129.1 54.9 all-gather.5
  185.7 405.1 all-gather.7
where the time goes:
time: 721 us; the launch traced here: 715 us
  waiting for transfers between devices  444 us (62%)
  local copies, waits for them, and re-layouts  128 us (18%)
  matrix products  99.4 us (14%)
  other arithmetic  20.2 us (3%)
  between operations  14.6 us (2%)
  blocking collectives  8.14 us (1%)
    all_gather x1, waiting for transfers between devices, channel_mix(): rows = lax.all_gather(weight, 'dp', axis=1, tiled=True)  328 us
    dot_general x10, matrix products, convolve(): jnp.dot(window, weight[shift], preferred_element_type=jnp.float32)  84.6 us
    all_gather x1, waiting for transfers between devices, body(): piece = lax.all_gather(film_weight, 'dp', axis=0, tiled=True)  61 us
    all_gather x1, waiting for transfers between devices, channel_mix(): return convolve(lax.all_gather(acts, 'tensor', axis=2, tiled=True), rows)  53.8 us
    slice x10, local copies, waits for them, and re-layouts, convolve(): window = padded[:, shift:shift + length, :].reshape(count * length, inner)  36.9 us
    reshape x9, local copies, waits for them, and re-layouts, convolve(): window = padded[:, shift:shift + length, :].reshape(count * length, inner)  36.2 us
    another operation x4, local copies, waits for them, and re-layouts, group_norm(): split = hidden.reshape(count, length, groups, width // groups)  22.9 us
    unnamed x45, local copies, waits for them, and re-layouts  19.5 us
  transfers between devices with their start and end apart: 3, of which 3 were waited for; matrix products, arithmetic and copies ran while one was open for 15% of the time, Pallas kernels for 0%

commit v1 on v0

v1 whole, which is shorter than its diff:
```python
import math

import jax
import jax.numpy as jnp
from jax import lax
from jax.experimental import pallas as pl
from jax.experimental.pallas import tpu as pltpu
from jax.sharding import Mesh
from jax.sharding import PartitionSpec as P

C = 4096
ACT = 7
HORIZON = 4
TAPS = 5
GROUPS = 8
STEP = 256
TRAIN_STEPS = 100


def plan():
    pos = jnp.arange(TRAIN_STEPS + 1, dtype=jnp.float32) / TRAIN_STEPS
    curve = jnp.cos((pos + 0.008) / 1.008 * (math.pi / 2)) ** 2
    betas = jnp.minimum(1.0 - curve[1:] / curve[:-1], 0.999)
    return jnp.cumprod(1.0 - betas)


def lookup(table, steps):
    onehot = (steps[:, None] == jnp.arange(table.shape[0], dtype=jnp.int32)[None, :]).astype(
        jnp.float32
    )
    return jnp.sum(onehot * table[None, :], axis=1)


def mish(value):
    e = jnp.exp(jnp.minimum(value, 20.0))
    n = e * (e + 2.0)
    return value * (n / (n + 2.0))


def sinusoid(steps):
    half = STEP // 2
    freqs = jnp.exp(jnp.arange(half, dtype=jnp.float32) * (-math.log(10000.0) / (half - 1)))
    angles = steps.astype(jnp.float32)[:, None] * freqs[None, :]
    return jnp.concatenate([jnp.sin(angles), jnp.cos(angles)], axis=1)


def denoise_step(sample, eps, noise, steps):
    alpha_bar = plan()
    now = lookup(alpha_bar, steps)[:, None]
    before = jnp.where(steps > 0, lookup(alpha_bar, jnp.maximum(steps - 1, 0)), 1.0)[:, None]
    beta_prod = 1.0 - now
    cur_alpha = now / before
    cur_beta = 1.0 - cur_alpha
    start = jnp.clip((sample - jnp.sqrt(beta_prod) * eps) / jnp.sqrt(now), -1.0, 1.0)
    mean = (
        jnp.sqrt(before) * cur_beta / beta_prod * start
        + jnp.sqrt(cur_alpha) * (1.0 - before) / beta_prod * sample
    )
    spread = jnp.sqrt((1.0 - before) / beta_prod * cur_beta)
    return mean + spread * noise


DEPTH_PARTS = 4
PARTS = 2
VMEM = 60 * 1024 * 1024


def first_kernel(blocks, x_ref, wt_ref, cond_ref, film_ref, gain_ref, out_ref):
    x = x_ref[...]
    hs = [
        jnp.dot(x, wt_ref[h], preferred_element_type=jnp.float32) for h in range(HORIZON)
    ]
    width = hs[0].shape[1]
    count = HORIZON * width
    mean = sum(jnp.sum(h, axis=1, keepdims=True) for h in hs) / count
    hs = [h - mean for h in hs]
    var = sum(jnp.sum(h * h, axis=1, keepdims=True) for h in hs) / count
    inv = 1.0 / jnp.sqrt(var + 1e-05)
    cond = cond_ref[...]
    scale = jnp.dot(cond, film_ref[0], preferred_element_type=jnp.float32)
    shift = jnp.dot(cond, film_ref[1], preferred_element_type=jnp.float32)
    gain = gain_ref[...]
    cl = width // blocks
    for h in range(HORIZON):
        val = (scale * mish(hs[h] * inv * gain) + shift).astype(jnp.bfloat16)
        for b in range(blocks):
            out_ref[b, :, h * cl : (h + 1) * cl] = val[:, b * cl : (b + 1) * cl]


def first_stage(xs, wt, cond, film, gain, blocks, cl):
    rows = xs.shape[0]
    width = wt.shape[2]
    gw = C // GROUPS
    per = gw // cl
    rt = min(128, rows)
    inner = cond.shape[1]
    kern = lambda *refs: first_kernel(per, *refs)
    return pl.pallas_call(
        kern,
        grid=(width // gw, rows // rt),
        in_specs=[
            pl.BlockSpec((rt, xs.shape[1]), lambda g, r: (r, 0)),
            pl.BlockSpec((HORIZON, wt.shape[1], gw), lambda g, r: (0, 0, g)),
            pl.BlockSpec((rt, inner), lambda g, r: (r, 0)),
            pl.BlockSpec((2, inner, gw), lambda g, r: (0, 0, g)),
            pl.BlockSpec((1, gw), lambda g, r: (0, g)),
        ],
        out_specs=pl.BlockSpec((per, rt, HORIZON * cl), lambda g, r: (g, r, 0)),
        out_shape=jax.ShapeDtypeStruct((blocks, rows, HORIZON * cl), jnp.bfloat16),
        compiler_params=pltpu.CompilerParams(vmem_limit_bytes=VMEM),
        cost_estimate=pl.CostEstimate(
            flops=4 * rows * inner * width,
            bytes_accessed=4 * inner * width + 2 * rows * width * HORIZON,
            transcendentals=rows * width * HORIZON,
        ),
        name="first_stage",
    )(xs, wt, cond, film, gain)


def mix_kernel(pieces, mid, order_ref, *refs):
    a_ref, w_refs, out_ref = refs[0], refs[1 : 1 + pieces], refs[1 + pieces]
    cl = w_refs[0].shape[0] // TAPS
    parts, _, rows, _ = out_ref.shape
    for h in range(HORIZON):
        p0 = max(0, h - mid)
        p1 = min(HORIZON, h - mid + TAPS)
        k0 = p0 - h + mid
        k1 = p1 - h + mid
        acc = None
        for i in range(pieces):
            left = a_ref[order_ref[i], :, p0 * cl : p1 * cl]
            term = jnp.dot(
                left, w_refs[i][k0 * cl : k1 * cl, :], preferred_element_type=jnp.float32
            )
            acc = term if acc is None else acc + term
        for q in range(parts):
            out_ref[q, h] = acc[q * rows : (q + 1) * rows].astype(jnp.bfloat16)


def mix(order, acts, pieces):
    n = len(pieces)
    rows = acts.shape[1]
    width = pieces[0].shape[1]
    nt = min(256, width)
    kern = lambda *refs: mix_kernel(n, TAPS // 2, *refs)
    return pl.pallas_call(
        kern,
        grid=(width // nt,),
        in_specs=[
            pl.BlockSpec(memory_space=pltpu.SMEM),
            pl.BlockSpec(acts.shape, lambda j: (0, 0, 0)),
        ]
        + [pl.BlockSpec((p.shape[0], nt), lambda j: (0, j)) for p in pieces],
        out_specs=pl.BlockSpec(
            (DEPTH_PARTS, HORIZON, rows // DEPTH_PARTS, nt), lambda j: (0, 0, 0, j)
        ),
        out_shape=jax.ShapeDtypeStruct(
            (DEPTH_PARTS, HORIZON, rows // DEPTH_PARTS, width), jnp.bfloat16
        ),
        compiler_params=pltpu.CompilerParams(vmem_limit_bytes=VMEM),
        cost_estimate=pl.CostEstimate(
            flops=2 * 14 * rows * n * pieces[0].shape[0] // TAPS * width,
            bytes_accessed=2 * n * pieces[0].shape[0] * width + 8 * rows * width,
            transcendentals=0,
        ),
        name="mix",
    )(order, acts, *pieces)


def hop(value, axis, step):
    size = lax.axis_size(axis)
    return lax.ppermute(value, axis, [(i, (i + step) % size) for i in range(size)])


def relative(value):
    return jnp.concatenate(
        [value] + [hop(value, "z", -q) for q in range(1, DEPTH_PARTS)], axis=0
    )


def reduce_parts(part):
    half = HORIZON // 2
    far = part[2]
    up = hop(far[:half], "z", 1)
    down = hop(far[half:], "z", -1)
    f32 = jnp.float32
    near_up = (part[1, :half].astype(f32) + up.astype(f32)).astype(jnp.bfloat16)
    near_down = (part[3, half:].astype(f32) + down.astype(f32)).astype(jnp.bfloat16)
    got = [
        (hop(near_up, "z", 1), hop(part[3, :half], "z", -1)),
        (hop(part[1, half:], "z", 1), hop(near_down, "z", -1)),
    ]
    out = []
    for h in range(HORIZON):
        one, two = got[h // half]
        out.append(
            part[0, h].astype(f32) + one[h % half].astype(f32) + two[h % half].astype(f32)
        )
    return out


def body(
    noisy_sample,
    timestep,
    noise,
    obs_feat,
    step_w1,
    step_w2,
    film_weight,
    conv_in_w,
    residual_w,
    conv_mid_w,
    out_w,
    gain_one,
    gain_two,
):
    count = noisy_sample.shape[0]
    local_width = conv_in_w.shape[2]
    cl = conv_mid_w.shape[1]
    yn = lax.axis_size("y")
    zi, yi, ci = lax.axis_index("z"), lax.axis_index("y"), lax.axis_index("c")
    blocks = yn * 2
    kw = cl * blocks
    step = local_width // PARTS
    pieces = []
    for n in range(PARTS):
        own = conv_mid_w.reshape(TAPS * cl, local_width)[:, n * step : (n + 1) * step]
        near = [own] + [hop(own, "y", -s) for s in range(1, yn)]
        pieces.append(near + [hop(v, "c", 1) for v in near])
    order = jnp.stack(
        [((yi + s) % yn) * 2 + ci for s in range(yn)]
        + [((yi + s) % yn) * 2 + (1 - ci) for s in range(yn)]
    ).astype(jnp.int32)
    film = jnp.transpose(film_weight, (1, 0, 2))
    film = lax.all_gather(film, "tensor", axis=2, tiled=True)
    film = lax.all_to_all(film, "z", split_axis=2, concat_axis=1, tiled=True)
    film = lax.all_gather(film, ("y", "c"), axis=1, tiled=True)
    win = lax.all_gather(conv_in_w, "tensor", axis=2, tiled=True)
    win = lax.dynamic_slice_in_dim(win, zi * kw, kw, 2)
    gain = lax.all_gather(gain_one, "tensor", axis=0, tiled=True)
    gain = lax.dynamic_slice_in_dim(gain, zi * kw, kw, 0)[None, :]
    toep = []
    for h in range(HORIZON):
        rows = []
        for p in range(HORIZON):
            k = p - h + TAPS // 2
            rows.append(win[k] if 0 <= k < TAPS else jnp.zeros((ACT, kw), win.dtype))
        toep.append(jnp.concatenate(rows, axis=0))
    toep = jnp.stack(toep)
    sample_b = noisy_sample.astype(jnp.bfloat16)
    sinus = sinusoid(timestep).astype(jnp.bfloat16)
    step_hidden = mish(jnp.dot(sinus, step_w1, preferred_element_type=jnp.float32)).astype(
        jnp.bfloat16
    )
    step_feat = jnp.dot(step_hidden, step_w2, preferred_element_type=jnp.float32)
    cond = mish(jnp.concatenate([step_feat, obs_feat.astype(jnp.float32)], axis=1)).astype(
        jnp.bfloat16
    )
    fr = film_weight.shape[0]
    cond = (
        cond.reshape(count, DEPTH_PARTS, blocks, fr)
        .transpose(0, 2, 1, 3)
        .reshape(count, cond.shape[1])
    )
    acts = first_stage(relative(sample_b), toep, relative(cond), film, gain, blocks, cl)
    found = [reduce_parts(mix(order, acts, p)) for p in pieces]
    hs = [jnp.concatenate([f[h] for f in found], axis=1) for h in range(HORIZON)]
    gw = C // GROUPS
    outs = []
    cols = [slice(g * gw, (g + 1) * gw) for g in range(local_width // gw)]
    stats = []
    for col in cols:
        mean = sum(jnp.sum(h[:, col], axis=1, keepdims=True) for h in hs) / (HORIZON * gw)
        var = sum(jnp.sum((h[:, col] - mean) ** 2, axis=1, keepdims=True) for h in hs) / (
            HORIZON * gw
        )
        stats.append((mean, 1.0 / jnp.sqrt(var + 1e-05)))
    mean = jnp.concatenate([jnp.broadcast_to(m, (count, gw)) for m, _ in stats], axis=1)
    inv = jnp.concatenate([jnp.broadcast_to(v, (count, gw)) for _, v in stats], axis=1)
    for h in range(HORIZON):
        skip = jnp.dot(
            sample_b[:, h * ACT : (h + 1) * ACT], residual_w, preferred_element_type=jnp.float32
        )
        normed = (hs[h] - mean) * inv * gain_two[None, :]
        act_two = (mish(normed) + skip).astype(jnp.bfloat16)
        outs.append(jnp.dot(act_two, out_w, preferred_element_type=jnp.float32))
    eps = lax.psum(jnp.concatenate(outs, axis=1), "tensor")
    denoised = denoise_step(noisy_sample, eps, noise, timestep)
    return (eps, denoised)


def solution(mesh):
    dp, tensor = mesh.shape["dp"], mesh.shape["tensor"]
    grid = Mesh(
        mesh.devices.reshape(DEPTH_PARTS, dp // DEPTH_PARTS // 2, 2, tensor),
        ("z", "y", "c", "tensor"),
    )
    rows = ("z", "y", "c")
    return jax.shard_map(
        body,
        mesh=grid,
        in_specs=(
            P(rows, None),
            P(rows),
            P(rows, None),
            P(rows, None),
            P(),
            P(),
            P(rows, None, "tensor"),
            P(None, None, "tensor"),
            P(None, "tensor"),
            P(None, rows, "tensor"),
            P("tensor", None),
            P("tensor"),
            P("tensor"),
        ),
        out_specs=(P(rows, None), P(rows, None)),
        check_vma=False,
    )
```

time: 721 us -> 473 us (0.66)
  waiting for transfers between devices: 444 us -> 220 us
  local copies, waits for them, and re-layouts: 128 us -> 32.6 us
  matrix products: 99.4 us -> 10.2 us
  blocking collectives: 8.14 us -> 70.3 us
  starting transfers between devices: 0.12 us -> 53.9 us
  Pallas kernels: 0 us -> 52.8 us
    all_gather x3 -> x2, waiting for transfers between devices: 443 us -> 27.1 us  [the longest x1 27.1 us: body(): film = lax.all_gather(film, 'tensor', axis=2, tiled=True)]
    ppermute x0 -> x24, waiting for transfers between devices: none -> 193 us  [hop(): lax.ppermute(value, axis, [(i, (i + step) % size) for i in range(size)])]
    dot_general x13 -> x4, matrix products: 97.8 us -> 8.52 us  [body(): outs.append(jnp.dot(act_two, out_w, preferred_element_type=jnp.float32))]
    ppermute x0 -> x24, starting transfers between devices: none -> 53.8 us  [hop(): lax.ppermute(value, axis, [(i, (i + step) % size) for i in range(size)])]
    pallas_call x0 -> x3, Pallas kernels: none -> 52.8 us  [the longest x2 40.5 us: mix(): pl.pallas_call(kern, grid=(width // nt,), in_specs=[pl.BlockSpec(memory_s...]
    all_to_all x0 -> x1, blocking collectives: none -> 52.5 us  [body(): film = lax.all_to_all(film, 'z', split_axis=2, concat_axis=1, tiled=True)]
    reshape x12 -> x1, local copies, waits for them, and re-layouts: 38.5 us -> 0.18 us  [body(): cond = cond.reshape(count, DEPTH_PARTS, blocks, fr).transpose(0, 2, 1, 3)...]
    slice x11 -> x3, local copies, waits for them, and re-layouts: 37.1 us -> 10.1 us  [the longest x2 5.56 us: reduce_parts(): up = hop(far[:half], 'z', 1)]
  transfers between devices with their start and end apart: 3 -> 26, of which waited for: 3 -> 12; matrix products, arithmetic and copies ran while one was open for 15% -> 6% of each run, Pallas kernels for 0% -> 11%
where the time goes in v1:
time: 473 us; the launch traced here: 472 us
  waiting for transfers between devices  220 us (47%)
  blocking collectives  70.3 us (15%)
  starting transfers between devices  53.9 us (11%)
  Pallas kernels  52.8 us (11%)
  local copies, waits for them, and re-layouts  32.6 us (7%)
  other arithmetic  17.7 us (4%)
  between operations  14.6 us (3%)
  matrix products  10.2 us (2%)
    ppermute x24, waiting for transfers between devices, hop(): lax.ppermute(value, axis, [(i, (i + step) % size) for i in range(size)])  193 us
    ppermute x24, starting transfers between devices, hop(): lax.ppermute(value, axis, [(i, (i + step) % size) for i in range(size)])  53.8 us
    all_to_all x1, blocking collectives, body(): film = lax.all_to_all(film, 'z', split_axis=2, concat_axis=1, tiled=True)  52.5 us
    pallas_call x2, Pallas kernels, mix(): pl.pallas_call(kern, grid=(width // nt,), in_specs=[pl.BlockSpec(memory_s...  40.5 us
    all_gather x1, waiting for transfers between devices, body(): film = lax.all_gather(film, 'tensor', axis=2, tiled=True)  27.1 us
    pallas_call x1, Pallas kernels, first_stage(): pl.pallas_call(kern, grid=(width // gw, rows // rt), in_specs=[pl.BlockSp...  12.3 us
  transfers between devices with their start and end apart: 26, of which 12 were waited for; matrix products, arithmetic and copies ran while one was open for 6% of the time, Pallas kernels for 11%

profile of v1, /device:TPU:0, one launch (start us, length us, event | category | flops | bytes accessed | tf_op | source)
XLA Modules:
  0.0 471.8 jit_solution(17640339304237799261)
XLA Ops:
  7.2 2.2 copy.67
  9.5 27.1 %all-gather.3.cloned.1.call-done = bf16[2,80,4096]{2,1,0:T(8,128)(2,1)} async-done(((bf16[2,80,2048]{2,1,0:T(8,128)(2,1)}), bf16[2,80,4096]{2,1,0:T(8,128)(2,1)}) %all-gather.3.cloned.1.call-update) | async-done | bytes 1310736 | tf_op jit(solution)/shard_map/all_gather | solution.py:235
  36.6 5.1 %copy.61 = bf16[2,80,4096]{1,0,2:T(2,128)(2,1)S(1)} copy(bf16[2,80,4096]{2,1,0:T(8,128)(2,1)} %all-gather.3.cloned.1.call-done) | data formatting | bytes 2621440 | tf_op jit(solution)/shard_map/all_gather | solution.py:235
  41.7 52.5 %all_to_all.18 = bf16[2,80,4096]{1,0,2:T(2,128)(2,1)} all-to-all(bf16[2,80,4096]{1,0,2:T(2,128)(2,1)S(1)} %copy.61), channel_id=1, replica_groups=mesh['z'=4,'y'=2,'c'=2,'tensor'=2] {'z'}, dimensions={2} | all-to-all | bytes 2621440 | tf_op jit(solution)/shard_map/all_to_all | solution.py:236
  94.2 6.0 %copy.62 = bf16[2,80,4,1024]{3,1,2,0:T(8,128)(2,1)} copy(bf16[2,80,4,1024]{1,0,3,2:T(2,128)(2,1)} %bitcast.203) | data formatting | bytes 2621440 | tf_op jit(solution)/shard_map/all_to_all | solution.py:236
  100.2 4.6 fusion.87
  104.8 1.5 collective-permute-start.12
  106.8 1.1 copy.53
  108.0 0.8 convert_element_type.226
  108.8 84.1 %collective-permute-done.12.refs_3_ = bf16[1280,1024]{1,0:T(8,128)(2,1)} collective-permute-done((bf16[1280,1024]{1,0:T(8,128)(2,1)}, bf16[1280,1024]{1,0:T(8,128)(2,1)}, u32[]{:S(2)}, u32[]{:S(2)}) %collective-permute-start.12) | collective-permute-done | bytes 2621472 | tf_op jit(solution)/shard_map/ppermute | solution.py:172
  193.9 1.6 fusion.48
  195.6 1.1 pad_maximum_fusion.3
  198.0 11.3 %collective-permute-done.2 = bf16[128,28]{0,1:T(8,128)(2,1)S(1)} collective-permute-done((bf16[128,28]{0,1:T(8,128)(2,1)S(1)}, bf16[128,28]{0,1:T(8,128)(2,1)S(1)}, u32[]{:S(2)}, u32[]{:S(2)}) %collective-permute-start.2) | collective-permute-done | bytes 7200 | tf_op jit(solution)/shard_map/ppermute | solution.py:172
  209.3 4.5 collective-permute-done.1
  213.9 6.0 %all_gather.12 = bf16[5,7,4096]{2,1,0:T(8,128)(2,1)S(1)} all-gather(bf16[5,7,2048]{2,1,0:T(8,128)(2,1)S(1)} %copy-done.11), channel_id=1, replica_groups=mesh['z'=4,'y'=2,'c'=2,'tensor'=2] {'tensor'}, dimensions={2}, use_global_device_ids=true | all-gather | bytes 430080 | tf_op jit(solution)/shard_map/all_gather | solution.py:238
  220.7 26.1 %collective-permute-done.6.refs_3_ = bf16[1280,1024]{1,0:T(8,128)(2,1)} collective-permute-done((bf16[1280,1024]{1,0:T(8,128)(2,1)S(1)}, bf16[1280,1024]{1,0:T(8,128)(2,1)}, u32[]{:S(2)}, u32[]{:S(2)}) %collective-permute-start.6) | collective-permute-done | bytes 2621472 | tf_op jit(solution)/shard_map/ppermute | solution.py:172
  247.4 4.6 all_gather.15
  252.5 2.3 collective-permute-start.3
  257.8 3.7 collective-permute-done.3
  261.5 2.2 pad_maximum_fusion.refs_2_
  263.7 12.3 %first_stage.1.refs_1_ = bf16[4,512,1024]{2,1,0:T(8,128)(2,1)} custom-call(bf16[512,28]{1,0:T(8,128)(2,1)} %copy.63.refs_0_, bf16[4,28,1024]{2,1,0:T(8,128)(2,1)} %pad_maximum_fusion.4.refs_1_, bf16[512,1280]{1,0:T(8,128)(2,1)} %pad_maximum_fusion.refs_2_, bf16[2,1280,1024]{2,1,0:T(8,128)(2,1)} %all-gather.5.cloned.1.call-done.refs_3_, f32[1,1024]{1,0:T(1,128)} %bitcast.209), custom_call_target="tpu_custom_call" | custom-call | flops 2684354560 | bytes 9437184 | tf_op jit(solution)/shard_map/first_stage/pallas_call | solution.py:98
  276.0 20.3 %mix.3 = bf16[4,4,128,1024]{3,2,1,0:T(8,128)(2,1)} custom-call(s32[4]{0:T(128)} %pad_add_fusion.refs_0_, bf16[4,512,1024]{2,1,0:T(8,128)(2,1)} %first_stage.1.refs_1_, bf16[1280,1024]{1,0:T(8,128)(2,1)} %get-tuple-element.56.refs_2_, bf16[1280,1024]{1,0:T(8,128)(2,1)} %collective-permute-done.12.refs_3_, bf16[1280,1024]{1,0:T(8,128)(2,1)} %collective-permute-done.13.refs_4_, ...), custom_call_target="tpu_custom_call" | custom-call | flops 15032385536 | bytes 14680064 | tf_op jit(solution)/shard_map/mix/pallas_call | solution.py:146
  296.3 2.9 slice_bitcast_fusion.7
  299.2 4.1 collective-permute-start.22
  303.3 20.2 %mix.2 = bf16[4,4,128,1024]{3,2,1,0:T(8,128)(2,1)} custom-call(s32[4]{0:T(128)} %pad_add_fusion.refs_0_, bf16[4,512,1024]{2,1,0:T(8,128)(2,1)} %first_stage.1.refs_1_, bf16[1280,1024]{1,0:T(8,128)(2,1)} %copy-done.4, bf16[1280,1024]{1,0:T(8,128)(2,1)} %collective-permute-done.6.refs_3_, bf16[1280,1024]{1,0:T(8,128)(2,1)} %collective-permute-done.7.refs_4_, ...), custom_call_target="tpu_custom_call" | custom-call | flops 15032385536 | bytes 14680064 | tf_op jit(solution)/shard_map/mix/pallas_call | solution.py:146
  323.6 2.6 slice_bitcast_fusion.10
  326.8 3.9 collective-permute-start.17
  330.7 3.8 collective-permute-start.19
  334.5 1.9 fusion.25
  336.5 6.6 %collective-permute-done.9 = bf16[2,128,1024]{2,1,0:T(8,128)(2,1)S(1)} collective-permute-done((bf16[2,128,1024]{2,1,0:T(8,128)(2,1)}, bf16[2,128,1024]{2,1,0:T(8,128)(2,1)S(1)}, u32[]{:S(2)}, u32[]{:S(2)}) %collective-permute-start.9) | collective-permute-done | bytes 524320 | tf_op jit(solution)/shard_map/ppermute | solution.py:172
  343.1 11.5 %collective-permute-start.23 = (bf16[2,128,1024]{2,1,0:T(8,128)(2,1)S(1)}, bf16[2,128,1024]{2,1,0:T(8,128)(2,1)S(1)}, u32[]{:S(2)}, u32[]{:S(2)}) collective-permute-start(bf16[2,128,1024]{2,1,0:T(8,128)(2,1)S(1)} %get-tuple-element.72), channel_id=1, source_target_pairs={{0,24},{8,0},{16,8},{24,16},{1,25},{9,1},{17,9},{25,17},{2,26},{10... | collective-permute-start | bytes 1572872 | tf_op jit(solution)/shard_map/ppermute | solution.py:172
  354.5 22.3 %collective-permute-done.19 = bf16[2,128,1024]{2,1,0:T(8,128)(2,1)S(1)} collective-permute-done((bf16[2,128,1024]{2,1,0:T(8,128)(2,1)S(1)}, bf16[2,128,1024]{2,1,0:T(8,128)(2,1)S(1)}, u32[]{:S(2)}, u32[]{:S(2)}) %collective-permute-start.19) | collective-permute-done | bytes 524320 | tf_op jit(solution)/shard_map/ppermute | solution.py:172
  376.9 1.6 fusion.26
  378.5 2.0 collective-permute-start.18
  381.1 7.0 %collective-permute-done.16 = bf16[2,128,1024]{2,1,0:T(8,128)(2,1)S(1)} collective-permute-done((bf16[2,128,1024]{2,1,0:T(8,128)(2,1)S(1)}, bf16[2,128,1024]{2,1,0:T(8,128)(2,1)S(1)}, u32[]{:S(2)}, u32[]{:S(2)}) %collective-permute-start.16) | collective-permute-done | bytes 524320 | tf_op jit(solution)/shard_map/ppermute | solution.py:172
  388.1 22.6 %collective-permute-start.20 = (bf16[2,128,1024]{2,1,0:T(8,128)(2,1)S(1)}, bf16[2,128,1024]{2,1,0:T(8,128)(2,1)S(1)}, u32[]{:S(2)}, u32[]{:S(2)}) collective-permute-start(bf16[2,128,1024]{2,1,0:T(8,128)(2,1)S(1)} %get-tuple-element.64), channel_id=1, source_target_pairs={{0,24},{8,0},{16,8},{24,16},{1,25},{9,1},{17,9},{25,17},{2,26},{10... | collective-permute-start | bytes 1572872 | tf_op jit(solution)/shard_map/ppermute | solution.py:172
  410.7 1.8 convert_add_fusion.8
  413.2 8.7 %collective-permute-done.18 = bf16[2,128,1024]{2,1,0:T(8,128)(2,1)S(1)} collective-permute-done((bf16[2,128,1024]{2,1,0:T(8,128)(2,1)S(1)}, bf16[2,128,1024]{2,1,0:T(8,128)(2,1)S(1)}, u32[]{:S(2)}, u32[]{:S(2)}) %collective-permute-start.18) | collective-permute-done | bytes 524320 | tf_op jit(solution)/shard_map/ppermute | solution.py:172
  421.9 11.2 %collective-permute-done.10 = bf16[2,128,1024]{2,1,0:T(8,128)(2,1)S(1)} collective-permute-done((bf16[2,128,1024]{2,1,0:T(8,128)(2,1)S(1)}, bf16[2,128,1024]{2,1,0:T(8,128)(2,1)S(1)}, u32[]{:S(2)}, u32[]{:S(2)}) %collective-permute-start.10) | collective-permute-done | bytes 524320 | tf_op jit(solution)/shard_map/ppermute | solution.py:172
  433.1 7.0 %collective-permute-done.20 = bf16[2,128,1024]{2,1,0:T(8,128)(2,1)S(1)} collective-permute-done((bf16[2,128,1024]{2,1,0:T(8,128)(2,1)S(1)}, bf16[2,128,1024]{2,1,0:T(8,128)(2,1)S(1)}, u32[]{:S(2)}, u32[]{:S(2)}) %collective-permute-start.20) | collective-permute-done | bytes 524320 | tf_op jit(solution)/shard_map/ppermute | solution.py:172
  440.1 1.7 convert_add_fusion.14
  442.7 0.8 broadcast_in_dim.28
  445.9 0.8 broadcast_in_dim.24
  448.3 2.3 fusion.4
  450.6 2.3 fusion.5
  453.1 2.0 fusion.6
  455.2 1.9 fusion.7
  457.1 7.2 %psum.7 = f32[128,28]{0,1:T(8,128)S(1)} all-reduce(f32[128,28]{0,1:T(8,128)S(1)} %pad_maximum_fusion.6), channel_id=1, replica_groups=mesh['z'=4,'y'=2,'c'=2,'tensor'=2] {'tensor'}, use_global_device_ids=true, to_apply=%region_32.33 | all-reduce | flops 3584 | bytes 28672 | tf_op jit(solution)/shard_map/psum | solution.py:287
  (131 shorter events, 15.3 us)
Async XLA Ops:
  7.2 186.7 %copy-start = (bf16[1024,256]{1,0:T(8,128)(2,1)S(1)}, bf16[1024,256]{1,0:T(8,128)(2,1)}, u32[]{:S(2)}) copy-start(bf16[1024,256]{1,0:T(8,128)(2,1)} %param.18) | copy-start | bytes 1572868
  7.2 29.4 %all-gather.3.cloned.1.call-start = ((), (), s32[]{:S(2)}) async-start(), calls=%async_computation.1 | async-start | bytes 1966080 | tf_op jit(solution)/shard_map/all_gather | solution.py:235
  9.5 254.3 %all-gather.5.cloned.1.call-start = ((), (), s32[]{:S(2)}) async-start(), calls=%async_computation.2 | async-start | bytes 6553600 | tf_op jit(solution)/shard_map/all_gather | solution.py:237
  100.2 92.8 %copy-start.20 = (s32[128]{0:T(128)S(1)}, s32[128]{0:T(128)}, u32[]{:S(2)}) copy-start(s32[128]{0:T(128)} %param.14) | copy-start | bytes 1540
  104.8 115.7 %copy-start.4 = (bf16[1280,1024]{1,0:T(8,128)(2,1)}, bf16[1280,1024]{1,0:T(8,128)(2,1)S(1)}, u32[]{:S(2)}) copy-start(bf16[1280,1024]{1,0:T(8,128)(2,1)S(1)} %get-tuple-element.55.refs_2_) | copy-start | bytes 7864324
  104.8 88.1 %collective-permute-start.12 = (bf16[1280,1024]{1,0:T(8,128)(2,1)}, bf16[1280,1024]{1,0:T(8,128)(2,1)}, u32[]{:S(2)}, u32[]{:S(2)}) collective-permute-start(bf16[1280,1024]{1,0:T(8,128)(2,1)} %get-tuple-element.56.refs_2_), channel_id=1, source_target_pairs={{0,4},{4,0},{1,5},{5,1},{2,6},{6,2},{3,7},{7,3},{8,12},{12,8},{9,1... | collective-permute-start | bytes 7864328 | tf_op jit(solution)/shard_map/ppermute | solution.py:172
  106.3 140.5 %collective-permute-start.6 = (bf16[1280,1024]{1,0:T(8,128)(2,1)S(1)}, bf16[1280,1024]{1,0:T(8,128)(2,1)}, u32[]{:S(2)}, u32[]{:S(2)}) collective-permute-start(bf16[1280,1024]{1,0:T(8,128)(2,1)S(1)} %get-tuple-element.55.refs_2_), channel_id=1, source_target_pairs={{0,4},{4,0},{1,5},{5,1},{2,6},{6,2},{3,7},{7,3},{8,12},{12,8},{9,1... | collective-permute-start | bytes 7864328 | tf_op jit(solution)/shard_map/ppermute | solution.py:172
  106.8 169.2 %collective-permute-start.13 = (bf16[1280,1024]{1,0:T(8,128)(2,1)}, bf16[1280,1024]{1,0:T(8,128)(2,1)}, u32[]{:S(2)}, u32[]{:S(2)}) collective-permute-start(bf16[1280,1024]{1,0:T(8,128)(2,1)} %get-tuple-element.56.refs_2_), channel_id=1, source_target_pairs={{0,2},{2,0},{1,3},{3,1},{4,6},{6,4},{5,7},{7,5},{8,10},{10,8},{9,1... | collective-permute-start | bytes 7864328 | tf_op jit(solution)/shard_map/ppermute | solution.py:172
  193.0 83.1 %collective-permute-start.14 = (bf16[1280,1024]{1,0:T(8,128)(2,1)}, bf16[1280,1024]{1,0:T(8,128)(2,1)}, u32[]{:S(2)}, u32[]{:S(2)}) collective-permute-start(bf16[1280,1024]{1,0:T(8,128)(2,1)} %collective-permute-done.12.refs_3_), channel_id=1, source_target_pairs={{0,2},{2,0},{1,3},{3,1},{4,6},{6,4},{5,7},{7,5},{8,10},{10,8},{9,1... | collective-permute-start | bytes 7864328 | tf_op jit(solution)/shard_map/ppermute | solution.py:172
  195.5 18.3 %copy-start.11 = (bf16[5,7,2048]{2,1,0:T(8,128)(2,1)S(1)}, bf16[5,7,2048]{2,1,0:T(8,128)(2,1)}, u32[]{:S(2)}) copy-start(bf16[5,7,2048]{2,1,0:T(8,128)(2,1)} %param.20) | copy-start | bytes 430084
  197.1 23.4 %collective-permute-start.5 = (bf16[128,1280]{1,0:T(8,128)(2,1)S(1)}, bf16[128,1280]{1,0:T(8,128)(2,1)}, u32[]{:S(2)}, u32[]{:S(2)}) collective-permute-start(bf16[128,1280]{1,0:T(8,128)(2,1)S(1)} %copy.59), channel_id=1, source_target_pairs={{0,8},{8,16},{16,24},{24,0},{1,9},{9,17},{17,25},{25,1},{2,10},{10... | collective-permute-start | bytes 983048 | tf_op jit(solution)/shard_map/ppermute | solution.py:172
  197.4 22.5 %copy-start.14 = (bf16[128,28]{0,1:T(8,128)(2,1)}, bf16[128,28]{0,1:T(8,128)(2,1)S(1)}, u32[]{:S(2)}) copy-start(bf16[128,28]{0,1:T(8,128)(2,1)S(1)} %convert_element_type.223) | copy-start | bytes 21508
  197.4 11.9 %collective-permute-start.2 = (bf16[128,28]{0,1:T(8,128)(2,1)S(1)}, bf16[128,28]{0,1:T(8,128)(2,1)S(1)}, u32[]{:S(2)}, u32[]{:S(2)}) collective-permute-start(bf16[128,28]{0,1:T(8,128)(2,1)S(1)} %convert_element_type.223), channel_id=1, source_target_pairs={{0,8},{8,16},{16,24},{24,0},{1,9},{9,17},{17,25},{25,1},{2,10},{10... | collective-permute-start | bytes 21512 | tf_op jit(solution)/shard_map/ppermute | solution.py:172
  209.3 10.6 %copy-start.17 = (bf16[128,28]{0,1:T(8,128)(2,1)}, bf16[128,28]{0,1:T(8,128)(2,1)S(1)}, u32[]{:S(2)}) copy-start(bf16[128,28]{0,1:T(8,128)(2,1)S(1)} %collective-permute-done.2) | copy-start | bytes 21508
  209.3 4.5 collective-permute-start.1
  213.8 6.1 %copy-start.18 = (bf16[128,28]{0,1:T(8,128)(2,1)}, bf16[128,28]{0,1:T(8,128)(2,1)S(1)}, u32[]{:S(2)}) copy-start(bf16[128,28]{0,1:T(8,128)(2,1)S(1)} %collective-permute-done.1) | copy-start | bytes 21508
  213.8 6.0 %collective-permute-start = (bf16[128,28]{0,1:T(8,128)(2,1)S(1)}, bf16[128,28]{0,1:T(8,128)(2,1)S(1)}, u32[]{:S(2)}, u32[]{:S(2)}) collective-permute-start(bf16[128,28]{0,1:T(8,128)(2,1)S(1)} %convert_element_type.223), channel_id=1, source_target_pairs={{0,24},{8,0},{16,8},{24,16},{1,25},{9,1},{17,9},{25,17},{2,26},{10... | collective-permute-start | bytes 21512 | tf_op jit(solution)/shard_map/ppermute | solution.py:172
  219.8 32.7 %collective-permute-start.4 = (bf16[128,1280]{1,0:T(8,128)(2,1)S(1)}, bf16[128,1280]{1,0:T(8,128)(2,1)}, u32[]{:S(2)}, u32[]{:S(2)}) collective-permute-start(bf16[128,1280]{1,0:T(8,128)(2,1)S(1)} %copy.59), channel_id=1, source_target_pairs={{0,16},{8,24},{16,0},{24,8},{1,17},{9,25},{17,1},{25,9},{2,18},{10... | collective-permute-start | bytes 983048 | tf_op jit(solution)/shard_map/ppermute | solution.py:172
  220.6 82.8 %collective-permute-start.7 = (bf16[1280,1024]{1,0:T(8,128)(2,1)S(1)}, bf16[1280,1024]{1,0:T(8,128)(2,1)}, u32[]{:S(2)}, u32[]{:S(2)}) collective-permute-start(bf16[1280,1024]{1,0:T(8,128)(2,1)S(1)} %get-tuple-element.55.refs_2_), channel_id=1, source_target_pairs={{0,2},{2,0},{1,3},{3,1},{4,6},{6,4},{5,7},{7,5},{8,10},{10,8},{9,1... | collective-permute-start | bytes 7864328 | tf_op jit(solution)/shard_map/ppermute | solution.py:172
  246.8 56.6 %collective-permute-start.8 = (bf16[1280,1024]{1,0:T(8,128)(2,1)}, bf16[1280,1024]{1,0:T(8,128)(2,1)}, u32[]{:S(2)}, u32[]{:S(2)}) collective-permute-start(bf16[1280,1024]{1,0:T(8,128)(2,1)} %collective-permute-done.6.refs_3_), channel_id=1, source_target_pairs={{0,2},{2,0},{1,3},{3,1},{4,6},{6,4},{5,7},{7,5},{8,10},{10,8},{9,1... | collective-permute-start | bytes 7864328 | tf_op jit(solution)/shard_map/ppermute | solution.py:172
  252.5 9.0 %collective-permute-start.3 = (bf16[128,1280]{1,0:T(8,128)(2,1)S(1)}, bf16[128,1280]{1,0:T(8,128)(2,1)S(1)}, u32[]{:S(2)}, u32[]{:S(2)}) collective-permute-start(bf16[128,1280]{1,0:T(8,128)(2,1)S(1)} %copy.59), channel_id=1, source_target_pairs={{0,24},{8,0},{16,8},{24,16},{1,25},{9,1},{17,9},{25,17},{2,26},{10... | collective-permute-start | bytes 983048 | tf_op jit(solution)/shard_map/ppermute | solution.py:172
  299.2 31.5 %collective-permute-start.15 = (bf16[2,128,1024]{2,1,0:T(8,128)(2,1)}, bf16[2,128,1024]{2,1,0:T(8,128)(2,1)}, u32[]{:S(2)}, u32[]{:S(2)}) collective-permute-start(bf16[2,128,1024]{2,1,0:T(8,128)(2,1)} %get-tuple-element.73), channel_id=1, source_target_pairs={{0,8},{8,16},{16,24},{24,0},{1,9},{9,17},{17,25},{25,1},{2,10},{10... | collective-permute-start | bytes 1572872 | tf_op jit(solution)/shard_map/ppermute | solution.py:172
  299.2 35.3 %collective-permute-start.22 = (bf16[2,128,1024]{2,1,0:T(8,128)(2,1)}, bf16[2,128,1024]{2,1,0:T(8,128)(2,1)}, u32[]{:S(2)}, u32[]{:S(2)}) collective-permute-start(bf16[2,128,1024]{2,1,0:T(8,128)(2,1)} %get-tuple-element.74), channel_id=1, source_target_pairs={{0,24},{8,0},{16,8},{24,16},{1,25},{9,1},{17,9},{25,17},{2,26},{10... | collective-permute-start | bytes 1572872 | tf_op jit(solution)/shard_map/ppermute | solution.py:172
  323.6 2.7 copy-start.25
  323.6 3.1 copy-start.21
  323.6 3.1 copy-start.22
  323.6 3.2 copy-start.6
  323.6 7.1 %copy-start.5 = (bf16[2,128,1024]{2,1,0:T(8,128)(2,1)S(1)}, bf16[2,128,1024]{2,1,0:T(8,128)(2,1)}, u32[]{:S(2)}) copy-start(bf16[2,128,1024]{2,1,0:T(8,128)(2,1)} %get-tuple-element.75) | copy-start | bytes 1572868
  326.2 16.8 %collective-permute-start.9 = (bf16[2,128,1024]{2,1,0:T(8,128)(2,1)}, bf16[2,128,1024]{2,1,0:T(8,128)(2,1)S(1)}, u32[]{:S(2)}, u32[]{:S(2)}) collective-permute-start(bf16[2,128,1024]{2,1,0:T(8,128)(2,1)} %get-tuple-element.65), channel_id=1, source_target_pairs={{0,8},{8,16},{16,24},{24,0},{1,9},{9,17},{17,25},{25,1},{2,10},{10... | collective-permute-start | bytes 1572872 | tf_op jit(solution)/shard_map/ppermute | solution.py:172
  326.8 51.6 %collective-permute-start.17 = (bf16[2,128,1024]{2,1,0:T(8,128)(2,1)S(1)}, bf16[2,128,1024]{2,1,0:T(8,128)(2,1)S(1)}, u32[]{:S(2)}, u32[]{:S(2)}) collective-permute-start(bf16[2,128,1024]{2,1,0:T(8,128)(2,1)S(1)} %copy-done.6), channel_id=1, source_target_pairs={{0,24},{8,0},{16,8},{24,16},{1,25},{9,1},{17,9},{25,17},{2,26},{10... | collective-permute-start | bytes 1572872 | tf_op jit(solution)/shard_map/ppermute | solution.py:172
  330.7 49.8 %collective-permute-start.21 = (bf16[2,128,1024]{2,1,0:T(8,128)(2,1)S(1)}, bf16[2,128,1024]{2,1,0:T(8,128)(2,1)S(1)}, u32[]{:S(2)}, u32[]{:S(2)}) collective-permute-start(bf16[2,128,1024]{2,1,0:T(8,128)(2,1)S(1)} %copy-done.5), channel_id=1, source_target_pairs={{0,8},{8,16},{16,24},{24,0},{1,9},{9,17},{17,25},{25,1},{2,10},{10... | collective-permute-start | bytes 1572872 | tf_op jit(solution)/shard_map/ppermute | solution.py:172
  330.7 46.1 %collective-permute-start.19 = (bf16[2,128,1024]{2,1,0:T(8,128)(2,1)S(1)}, bf16[2,128,1024]{2,1,0:T(8,128)(2,1)S(1)}, u32[]{:S(2)}, u32[]{:S(2)}) collective-permute-start(bf16[2,128,1024]{2,1,0:T(8,128)(2,1)S(1)} %get-tuple-element.66), channel_id=1, source_target_pairs={{0,24},{8,0},{16,8},{24,16},{1,25},{9,1},{17,9},{25,17},{2,26},{10... | collective-permute-start | bytes 1572872 | tf_op jit(solution)/shard_map/ppermute | solution.py:172
  336.4 51.7 %collective-permute-start.16 = (bf16[2,128,1024]{2,1,0:T(8,128)(2,1)S(1)}, bf16[2,128,1024]{2,1,0:T(8,128)(2,1)S(1)}, u32[]{:S(2)}, u32[]{:S(2)}) collective-permute-start(bf16[2,128,1024]{2,1,0:T(8,128)(2,1)S(1)} %get-tuple-element.71), channel_id=1, source_target_pairs={{0,8},{8,16},{16,24},{24,0},{1,9},{9,17},{17,25},{25,1},{2,10},{10... | collective-permute-start | bytes 1572872 | tf_op jit(solution)/shard_map/ppermute | solution.py:172
  343.1 67.6 %collective-permute-start.23 = (bf16[2,128,1024]{2,1,0:T(8,128)(2,1)S(1)}, bf16[2,128,1024]{2,1,0:T(8,128)(2,1)S(1)}, u32[]{:S(2)}, u32[]{:S(2)}) collective-permute-start(bf16[2,128,1024]{2,1,0:T(8,128)(2,1)S(1)} %get-tuple-element.72), channel_id=1, source_target_pairs={{0,24},{8,0},{16,8},{24,16},{1,25},{9,1},{17,9},{25,17},{2,26},{10... | collective-permute-start | bytes 1572872 | tf_op jit(solution)/shard_map/ppermute | solution.py:172
  376.8 36.3 %collective-permute-start.11 = (bf16[2,128,1024]{2,1,0:T(8,128)(2,1)S(1)}, bf16[2,128,1024]{2,1,0:T(8,128)(2,1)S(1)}, u32[]{:S(2)}, u32[]{:S(2)}) collective-permute-start(bf16[2,128,1024]{2,1,0:T(8,128)(2,1)S(1)} %get-tuple-element.68), channel_id=1, source_target_pairs={{0,24},{8,0},{16,8},{24,16},{1,25},{9,1},{17,9},{25,17},{2,26},{10... | collective-permute-start | bytes 1572872 | tf_op jit(solution)/shard_map/ppermute | solution.py:172
  378.5 43.4 %collective-permute-start.18 = (bf16[2,128,1024]{2,1,0:T(8,128)(2,1)S(1)}, bf16[2,128,1024]{2,1,0:T(8,128)(2,1)S(1)}, u32[]{:S(2)}, u32[]{:S(2)}) collective-permute-start(bf16[2,128,1024]{2,1,0:T(8,128)(2,1)S(1)} %get-tuple-element.67), channel_id=1, source_target_pairs={{0,8},{8,16},{16,24},{24,0},{1,9},{9,17},{17,25},{25,1},{2,10},{10... | collective-permute-start | bytes 1572872 | tf_op jit(solution)/shard_map/ppermute | solution.py:172
  380.5 52.6 %collective-permute-start.10 = (bf16[2,128,1024]{2,1,0:T(8,128)(2,1)S(1)}, bf16[2,128,1024]{2,1,0:T(8,128)(2,1)S(1)}, u32[]{:S(2)}, u32[]{:S(2)}) collective-permute-start(bf16[2,128,1024]{2,1,0:T(8,128)(2,1)S(1)} %get-tuple-element.63), channel_id=1, source_target_pairs={{0,8},{8,16},{16,24},{24,0},{1,9},{9,17},{17,25},{25,1},{2,10},{10... | collective-permute-start | bytes 1572872 | tf_op jit(solution)/shard_map/ppermute | solution.py:172
  388.1 52.0 %collective-permute-start.20 = (bf16[2,128,1024]{2,1,0:T(8,128)(2,1)S(1)}, bf16[2,128,1024]{2,1,0:T(8,128)(2,1)S(1)}, u32[]{:S(2)}, u32[]{:S(2)}) collective-permute-start(bf16[2,128,1024]{2,1,0:T(8,128)(2,1)S(1)} %get-tuple-element.64), channel_id=1, source_target_pairs={{0,24},{8,0},{16,8},{24,16},{1,25},{9,1},{17,9},{25,17},{2,26},{10... | collective-permute-start | bytes 1572872 | tf_op jit(solution)/shard_map/ppermute | solution.py:172
  441.8 3.3 copy-start.2
  441.8 3.3 copy-start.3
  442.0 6.3 %copy-start.15 = (bf16[128,28]{0,1:T(8,128)(2,1)S(1)}, bf16[128,28]{0,1:T(8,128)(2,1)}, u32[]{:S(2)}) copy-start(bf16[128,28]{0,1:T(8,128)(2,1)} %copy-done.14) | copy-start | bytes 21508
  442.0 6.3 %copy-start.24 = (f32[2048]{0:T(1024)S(1)}, f32[2048]{0:T(1024)}, u32[]{:S(2)}) copy-start(f32[2048]{0:T(1024)} %param.25) | copy-start | bytes 24580
  448.3 2.3 copy-start.23
  450.6 2.4 copy-start.7
  450.6 2.4 copy-start.8
  453.0 2.0 copy-start.10
  455.1 9.2 %copy-start.16 = (f32[128,28]{0,1:T(8,128)S(1)}, f32[128,28]{0,1:T(8,128)}, u32[]{:S(2)}) copy-start(f32[128,28]{0,1:T(8,128)} %param.15) | copy-start | bytes 43012
  455.1 9.8 %copy-start.1 = (bf16[1024,256]{1,0:T(8,128)(2,1)S(1)}, bf16[1024,256]{1,0:T(8,128)(2,1)}, u32[]{:S(2)}) copy-start(bf16[1024,256]{1,0:T(8,128)(2,1)} %param.18) | copy-start | bytes 1572868
  (4 other events, 5.1 us)
Sparse Core Ops, SparseCore 0:
  9.6 26.9 all-gather.2
  100.3 66.7 all-gather.4
